TPU v7x, 32 devices: a whole 2x2x4 slice. The times are simulated.
32 devices in a mesh: groups: 2 (over y), slab: 4 (over z), pencil: 2 (over x), comp: 2 (over core).
Axes of the slice: x: 2, y: 2, z: 4, core: 2. Of those that a mesh axis runs over, the one named last changes fastest.
Arguments:
- u_start: float32 [3, 64, 64, 512], P(None, ('groups', 'slab'), 'pencil', 'comp'), parts along dimension 1, may hold values from -6 to 6
- toughness: float32 [64, 64, 512], P(('groups', 'slab'), 'pencil', 'comp'), parts along dimension 0, may hold values from 0.3 to 1.5
- crack_label: int32 [64, 64, 512], P(('groups', 'slab'), 'pencil', 'comp'), parts along dimension 0, may hold values from 0 to 2
- obs_weight: bfloat16 [32, 64, 2, 4096], P('slab', 'pencil', 'comp'), may hold values from -0.75 to 0.75
- sensor_cell: int32 [4096], replicated, may hold values from 0 to 4095
Outputs:
- moved: float32 [3, 64, 64, 512], P(None, ('groups', 'slab'), 'pencil', 'comp'), parts along dimension 1
- damage: float32 [64, 64, 512], P(('groups', 'slab'), 'pencil', 'comp'), parts along dimension 0
- readings: float32 [3, 8192], P(None, 'groups'), parts along dimension 1
There are 2 independent parts, one for each index of `groups`. A program takes and returns all parts, laid end to end along the dimension named above; an argument that names none is the same for every part. Nothing has to cross between parts.
Inputs may be any that keep to these rules, and one draw needn't show every extreme that they name: `sensor_cell`: numbers cell blocks as (64 z + y) * 2 + h. `crack_label`: 0 intact, 1 partly cracked, 2 cracked.
All inputs are finite; a program needn't handle non-finite values.
Results may differ from a plain program's by a relative error of at most 0.003.
Values sent between devices are 32-bit elements; how exact they have to be, the bound alone decides.
A program may use at most 128 MiB of HBM per device.

v0:
```python
import jax
import jax.numpy as jnp
from jax import lax
from jax.sharding import PartitionSpec as P

SHEAR_MODULUS = 1.0
LAME_FIRST = 1.5
RESIDUAL_STIFF = 0.001
TIME_DISP = 0.15
TIME_DAMAGE = 0.08
LENGTH_SCALE = 1.0
DAMAGE_LEVEL = 0.45
POINT_GAIN = 8.0


def with_halo(block, sides, width):
    for axis, dim in sides:
        count = lax.axis_size(axis)
        forward = [(i, i + 1) for i in range(count - 1)]
        backward = [(target, source) for source, target in forward]
        low = lax.ppermute(
            lax.slice_in_dim(block, block.shape[dim] - width, None, axis=dim), axis, forward
        )
        high = lax.ppermute(lax.slice_in_dim(block, 0, width, axis=dim), axis, backward)
        block = jnp.concatenate([low, block, high], axis=dim)
    return block


def central(source, spatial):
    if spatial == 0:
        return 0.5 * (source[..., 2:, 1:-1, 1:-1] - source[..., :-2, 1:-1, 1:-1])
    if spatial == 1:
        return 0.5 * (source[..., 1:-1, 2:, 1:-1] - source[..., 1:-1, :-2, 1:-1])
    return 0.5 * (source[..., 1:-1, 1:-1, 2:] - source[..., 1:-1, 1:-1, :-2])


def shrink(source):
    return source[..., 1:-1, 1:-1, 1:-1]


def laplace(source):
    return (
        source[2:, 1:-1, 1:-1]
        + source[:-2, 1:-1, 1:-1]
        + source[1:-1, 2:, 1:-1]
        + source[1:-1, :-2, 1:-1]
        + source[1:-1, 1:-1, 2:]
        + source[1:-1, 1:-1, :-2]
        - 6.0 * source[1:-1, 1:-1, 1:-1]
    )


def entry_key(first, second):
    return (min(first, second), max(first, second))


def rotate(matrix, first, second):
    other = 3 - first - second
    diag_first = matrix[first, first]
    diag_second = matrix[second, second]
    coupling = matrix[first, second]
    angle = 0.5 * jnp.arctan2(2.0 * coupling, diag_second - diag_first)
    cosine = jnp.cos(angle)
    sine = jnp.sin(angle)
    side_first = matrix[entry_key(other, first)]
    side_second = matrix[entry_key(other, second)]
    result = dict(matrix)
    result[first, first] = (
        cosine * cosine * diag_first - 2.0 * cosine * sine * coupling + sine * sine * diag_second
    )
    result[second, second] = (
        sine * sine * diag_first + 2.0 * cosine * sine * coupling + cosine * cosine * diag_second
    )
    result[first, second] = jnp.zeros_like(coupling)
    result[entry_key(other, first)] = cosine * side_first - sine * side_second
    result[entry_key(other, second)] = sine * side_first + cosine * side_second
    return result


def eigenvalues(matrix):
    for sweep_index in range(5):
        for first, second in ((0, 1), (0, 2), (1, 2)):
            matrix = rotate(matrix, first, second)
    return [matrix[0, 0], matrix[1, 1], matrix[2, 2]]


def advance(padded_disp, padded_damage, toughness):
    gradient = [
        [central(padded_disp[component], direction) for direction in range(3)]
        for component in range(3)
    ]
    strain = {}
    for first in range(3):
        for second in range(first, 3):
            strain[first, second] = 0.5 * (gradient[first][second] + gradient[second][first])
    trace_full = strain[0, 0] + strain[1, 1] + strain[2, 2]
    damage_mid = shrink(padded_damage)
    degrade = (1.0 - damage_mid) ** 2 + RESIDUAL_STIFF
    divergence = []
    for component in range(3):
        total_force = 0.0
        for direction in range(3):
            stress = 2.0 * SHEAR_MODULUS * strain[entry_key(component, direction)]
            if component == direction:
                stress = stress + LAME_FIRST * trace_full
            total_force = total_force + central(degrade * stress, direction)
        divergence.append(total_force)
    moved = shrink(shrink(padded_disp)) + TIME_DISP * jnp.stack(divergence)
    inner = {key_pair: shrink(entry_value) for key_pair, entry_value in strain.items()}
    trace_inner = shrink(trace_full)
    energy = 0.5 * LAME_FIRST * jnp.maximum(trace_inner, 0.0) ** 2
    for eigen_value in eigenvalues(inner):
        energy = energy + SHEAR_MODULUS * jnp.maximum(eigen_value, 0.0) ** 2
    damage_core = shrink(damage_mid)
    damage = damage_core + TIME_DAMAGE * (
        2.0 * (1.0 - damage_core) * energy
        - toughness / LENGTH_SCALE * damage_core
        + toughness * LENGTH_SCALE * laplace(damage_mid)
    )
    return (moved, damage)


def local(u_start, toughness, crack_label, obs_weight, sensor_cell):
    planes, rows, columns = toughness.shape
    damage = DAMAGE_LEVEL * crack_label.astype(jnp.float32)
    moved = u_start
    for repeat in range(2):
        stacked = jnp.concatenate([moved, damage[None]], axis=0)
        padded = with_halo(stacked, (("slab", 1), ("pencil", 2), ("comp", 3)), 2)
        moved, damage = advance(padded[:3], padded[3], toughness)
    pooled = jnp.mean(moved, axis=-1).reshape(3, planes * rows).astype(jnp.bfloat16)
    weight_rows = obs_weight.reshape(planes * rows, obs_weight.shape[-1])
    dense = jnp.dot(pooled, weight_rows, preferred_element_type=jnp.float32)
    plane_ids = lax.axis_index("slab") * planes + jnp.arange(planes, dtype=jnp.int32)
    row_ids = lax.axis_index("pencil") * rows + jnp.arange(rows, dtype=jnp.int32)
    block_ids = (
        (plane_ids[:, None] * (rows * lax.axis_size("pencil")) + row_ids[None, :])
        * lax.axis_size("comp")
        + lax.axis_index("comp")
    ).reshape(planes * rows)
    picks = (block_ids[:, None] == sensor_cell[None, :]).astype(jnp.bfloat16)
    point = jnp.dot(pooled, picks, preferred_element_type=jnp.float32)
    partial_sum = dense + POINT_GAIN * point
    readings = lax.psum(partial_sum, ("slab", "pencil", "comp"))
    return (moved, damage, readings)


def solution(mesh):
    return jax.shard_map(
        local,
        mesh=mesh,
        in_specs=(
            P(None, ("groups", "slab"), "pencil", "comp"),
            P(("groups", "slab"), "pencil", "comp"),
            P(("groups", "slab"), "pencil", "comp"),
            P("slab", "pencil", "comp", None),
            P(),
        ),
        out_specs=(
            P(None, ("groups", "slab"), "pencil", "comp"),
            P(("groups", "slab"), "pencil", "comp"),
            P(None, "groups"),
        ),
        check_vma=False,
    )
```

profile of v0, /device:TPU:0, one launch (start us, length us, event | category | flops | bytes accessed | tf_op | source)
XLA Modules:
  0.0 226.6 jit_solution(18250146474018214217)
XLA Ops:
  2.9 5.0 %collective-permute-start = (f32[4,2,32,256]{3,2,1,0:T(8,128)S(1)}, f32[4,2,32,256]{3,2,1,0:T(8,128)S(1)}, u32[]{:S(2)}, u32[]{:S(2)}) collective-permute-start(f32[4,2,32,256]{3,2,1,0:T(8,128)S(1)} %get-tuple-element.66), channel_id=1, source_target_pairs={{0,4},{4,8},{8,12},{1,5},{5,9},{9,13},{2,6},{6,10},{10,14},{3,7},{... | collective-permute-start | bytes 786440 | tf_op jit(solution)/shard_map/ppermute | solution.py:21
  9.1 4.2 %collective-permute-done = f32[4,2,32,256]{3,2,1,0:T(8,128)S(1)} collective-permute-done((f32[4,2,32,256]{3,2,1,0:T(8,128)S(1)}, f32[4,2,32,256]{3,2,1,0:T(8,128)S(1)}, u32[]{:S(2)}, u32[]{:S(2)}) %collective-permute-start) | collective-permute-done | bytes 262176 | tf_op jit(solution)/shard_map/ppermute | solution.py:21
  13.4 4.1 %collective-permute-done.1 = f32[4,2,32,256]{3,2,1,0:T(8,128)S(1)} collective-permute-done((f32[4,2,32,256]{3,2,1,0:T(8,128)S(1)}, f32[4,2,32,256]{3,2,1,0:T(8,128)S(1)}, u32[]{:S(2)}, u32[]{:S(2)}) %collective-permute-start.1) | collective-permute-done | bytes 262176 | tf_op jit(solution)/shard_map/ppermute | solution.py:24
  18.7 3.4 %collective-permute-start.2 = (f32[4,12,2,256]{3,2,1,0:T(2,128)S(1)}, f32[4,12,2,256]{3,2,1,0:T(2,128)S(1)}, u32[]{:S(2)}, u32[]{:S(2)}) collective-permute-start(f32[4,12,2,256]{3,2,1,0:T(2,128)S(1)} %get-tuple-element.58), channel_id=1, source_target_pairs={{0,2},{1,3},{4,6},{5,7},{8,10},{9,11},{12,14},{13,15},{16,18},{17,... | collective-permute-start | bytes 294920 | tf_op jit(solution)/shard_map/ppermute | solution.py:21
  24.3 4.3 %collective-permute-done.3 = f32[4,12,2,256]{3,2,1,0:T(2,128)S(1)} collective-permute-done((f32[4,12,2,256]{3,2,1,0:T(2,128)S(1)}, f32[4,12,2,256]{3,2,1,0:T(2,128)S(1)}, u32[]{:S(2)}, u32[]{:S(2)}) %collective-permute-start.3) | collective-permute-done | bytes 98336 | tf_op jit(solution)/shard_map/ppermute | solution.py:24
  28.9 1.6 fusion.80
  30.5 1.6 copy.24
  32.2 1.9 collective-permute-start.4
  34.1 2.2 copy.25
  37.6 2.2 copy.26
  39.8 2.2 copy.27
  42.0 3.1 %pad_maximum_fusion = f32[4,12,36,260]{3,2,1,0:T(8,128)S(1)} fusion(f32[4,12,36,2]{3,2,1,0:T(8,128)} %copy.27, f32[4,12,2,256]{3,2,1,0:T(2,128)} %copy-done.13, f32[4,2,32,256]{3,2,1,0:T(8,128)} %copy-done.5, f32[1,8,32,256]{3,2,1,0:T(8,128)S(1)} %multiply_bitcast_fusion, f32[3,8,32,256]{3,2,1,0:T(8,128)S(1)} %copy-done.1, ...), kind=kLoop, calls=%fused_computation.3 | loop fusion | flops 3144960 | bytes 3594240 | tf_op jit(solution)/shard_map/concatenate | solution.py:25
  45.3 2.2 multiply_multiply_fusion.5
  50.1 29.3 %fusion.51 = f32[1,8,32,256]{3,2,1,0:T(8,128)S(1)} fusion(f32[8,32,256]{2,1,0:T(8,128)S(1)} %copy-done.15, f32[12,36,260]{2,1,0:T(8,128)S(1)} %get-tuple-element.37, f32[10,34,258]{2,1,0:T(8,128)S(1)} %get-tuple-element.46, f32[10,34,258]{2,1,0:T(8,128)S(1)} %get-tuple-element.47, f32[10,34,258]{2,1,0:T(8,128)S(1)} %get-tuple-element.29, ...), kind=kLoop, calls=%fused_computation.127 | loop fusion | flops 23068672 | bytes 4194304 | tf_op jit(solution)/shard_map/broadcast_in_dim | solution.py:128
  80.3 3.5 %collective-permute-start.6 = (f32[4,2,32,256]{3,2,1,0:T(8,128)}, f32[4,2,32,256]{3,2,1,0:T(8,128)S(1)}, u32[]{:S(2)}, u32[]{:S(2)}) collective-permute-start(f32[4,2,32,256]{3,2,1,0:T(8,128)} %get-tuple-element.64), channel_id=1, source_target_pairs={{0,4},{4,8},{8,12},{1,5},{5,9},{9,13},{2,6},{6,10},{10,14},{3,7},{... | collective-permute-start | bytes 786440 | tf_op jit(solution)/shard_map/ppermute | solution.py:21
  85.7 4.3 %collective-permute-done.6 = f32[4,2,32,256]{3,2,1,0:T(8,128)S(1)} collective-permute-done((f32[4,2,32,256]{3,2,1,0:T(8,128)}, f32[4,2,32,256]{3,2,1,0:T(8,128)S(1)}, u32[]{:S(2)}, u32[]{:S(2)}) %collective-permute-start.6) | collective-permute-done | bytes 262176 | tf_op jit(solution)/shard_map/ppermute | solution.py:21
  90.0 4.7 %collective-permute-done.7 = f32[4,2,32,256]{3,2,1,0:T(8,128)} collective-permute-done((f32[4,2,32,256]{3,2,1,0:T(8,128)}, f32[4,2,32,256]{3,2,1,0:T(8,128)}, u32[]{:S(2)}, u32[]{:S(2)}) %collective-permute-start.7) | collective-permute-done | bytes 262176 | tf_op jit(solution)/shard_map/ppermute | solution.py:24
  95.9 1.5 collective-permute-start.8
  100.0 4.1 %collective-permute-done.9 = f32[4,12,2,256]{3,2,1,0:T(2,128)S(1)} collective-permute-done((f32[4,12,2,256]{3,2,1,0:T(2,128)S(1)}, f32[4,12,2,256]{3,2,1,0:T(2,128)S(1)}, u32[]{:S(2)}, u32[]{:S(2)}) %collective-permute-start.9) | collective-permute-done | bytes 98336 | tf_op jit(solution)/shard_map/ppermute | solution.py:24
  104.1 1.5 pad_maximum_fusion.3
  105.6 1.6 fusion.79
  107.2 1.6 copy.28
  108.8 1.9 collective-permute-start.10
  110.7 2.2 copy.29
  117.0 2.2 copy.30
  119.2 2.2 copy.31
  121.4 3.3 %pad_maximum_fusion.1 = f32[4,12,36,260]{3,2,1,0:T(8,128)S(1)} fusion(f32[4,12,36,2]{3,2,1,0:T(8,128)} %copy.31, f32[4,12,2,256]{3,2,1,0:T(2,128)} %copy-done.12, f32[4,2,32,256]{3,2,1,0:T(8,128)} %collective-permute-done.7, f32[1,8,32,256]{3,2,1,0:T(8,128)S(1)} %fusion.51, f32[3,8,32,256]{3,2,1,0:T(8,128)} %copy-done.2, ...), kind=kLoop, calls=%fused_computation.4 | loop fusion | flops 3144960 | bytes 3594240 | tf_op jit(solution)/shard_map/concatenate | solution.py:25
  124.9 3.8 %multiply_multiply_fusion.2 = (f32[10,34,258]{2,1,0:T(8,128)S(1)}, f32[10,34,258]{2,1,0:T(8,128)}, f32[10,34,258]{2,1,0:T(8,128)S(1)}, f32[10,34,258]{2,1,0:T(8,...) fusion(f32[12,36,260]{2,1,0:T(8,128)S(1)} %get-tuple-element.33, ...), kind=kLoop, calls=%fused_computation.61 | loop fusion | flops 2456160 | bytes 8421120 | tf_op jit(solution)/shard_map/mul | solution.py:106
  128.7 2.1 multiply_multiply_fusion
  133.6 1.4 fusion
  135.0 60.5 %psum.7 = f32[3,4096]{1,0:T(4,128)} all-reduce(f32[3,4096]{1,0:T(4,128)} %fusion), channel_id=1, replica_groups=mesh['groups'=2,'slab'=4,'pencil'=2,'comp'=2] {'slab','pencil','comp'}, use_global_device_ids=true, to_apply=%region_1.0 | all-reduce | flops 12288 | bytes 98304 | tf_op jit(solution)/shard_map/psum | solution.py:144
  195.5 31.0 %fusion.26 = f32[8,32,256]{2,1,0:T(8,128)} fusion(f32[8,32,256]{2,1,0:T(8,128)} %param.6, f32[12,36,260]{2,1,0:T(8,128)S(1)} %copy-done.4, f32[10,34,258]{2,1,0:T(8,128)S(1)} %get-tuple-element.39, f32[10,34,258]{2,1,0:T(8,128)} %get-tuple-element.40, f32[10,34,258]{2,1,0:T(8,128)} %get-tuple-element.18, f32[10,34,258]{2,1,0:T(8,128)} %get-tuple-element.44, ...), kind=kLoop, calls=%fused_computation.82 | loop fusion | flops 23068672 | bytes 4194304 | tf_op jit(solution)/shard_map/add | solution.py:115
  (66 shorter events, 24.4 us)
Async XLA Ops:
  0.6 132.5 %copy-start = (bf16[8,32,1,4096]{3,1,2,0:T(8,128)(2,1)S(1)}, bf16[8,32,1,4096]{3,1,2,0:T(8,128)(2,1)}, u32[]{:S(2)}) copy-start(bf16[8,32,1,4096]{3,1,2,0:T(8,128)(2,1)} %param.8) | copy-start | bytes 6291460
  0.6 28.0 %copy-start.1 = (f32[3,8,32,256]{3,2,1,0:T(8,128)S(1)}, f32[3,8,32,256]{3,2,1,0:T(8,128)}, u32[]{:S(2)}) copy-start(f32[3,8,32,256]{3,2,1,0:T(8,128)} %param.5) | copy-start | bytes 2359300
  2.9 10.5 %collective-permute-start = (f32[4,2,32,256]{3,2,1,0:T(8,128)S(1)}, f32[4,2,32,256]{3,2,1,0:T(8,128)S(1)}, u32[]{:S(2)}, u32[]{:S(2)}) collective-permute-start(f32[4,2,32,256]{3,2,1,0:T(8,128)S(1)} %get-tuple-element.66), channel_id=1, source_target_pairs={{0,4},{4,8},{8,12},{1,5},{5,9},{9,13},{2,6},{6,10},{10,14},{3,7},{... | collective-permute-start | bytes 786440 | tf_op jit(solution)/shard_map/ppermute | solution.py:21
  7.8 9.7 %collective-permute-start.1 = (f32[4,2,32,256]{3,2,1,0:T(8,128)S(1)}, f32[4,2,32,256]{3,2,1,0:T(8,128)S(1)}, u32[]{:S(2)}, u32[]{:S(2)}) collective-permute-start(f32[4,2,32,256]{3,2,1,0:T(8,128)S(1)} %get-tuple-element.67), channel_id=1, source_target_pairs={{4,0},{8,4},{12,8},{5,1},{9,5},{13,9},{6,2},{10,6},{14,10},{7,3},{... | collective-permute-start | bytes 786440 | tf_op jit(solution)/shard_map/ppermute | solution.py:24
  17.5 13.0 %copy-start.5 = (f32[4,2,32,256]{3,2,1,0:T(8,128)}, f32[4,2,32,256]{3,2,1,0:T(8,128)S(1)}, u32[]{:S(2)}) copy-start(f32[4,2,32,256]{3,2,1,0:T(8,128)S(1)} %collective-permute-done.1) | copy-start | bytes 786436
  18.7 5.6 %collective-permute-start.2 = (f32[4,12,2,256]{3,2,1,0:T(2,128)S(1)}, f32[4,12,2,256]{3,2,1,0:T(2,128)S(1)}, u32[]{:S(2)}, u32[]{:S(2)}) collective-permute-start(f32[4,12,2,256]{3,2,1,0:T(2,128)S(1)} %get-tuple-element.58), channel_id=1, source_target_pairs={{0,2},{1,3},{4,6},{5,7},{8,10},{9,11},{12,14},{13,15},{16,18},{17,... | collective-permute-start | bytes 294920 | tf_op jit(solution)/shard_map/ppermute | solution.py:21
  22.1 6.5 %collective-permute-start.3 = (f32[4,12,2,256]{3,2,1,0:T(2,128)S(1)}, f32[4,12,2,256]{3,2,1,0:T(2,128)S(1)}, u32[]{:S(2)}, u32[]{:S(2)}) collective-permute-start(f32[4,12,2,256]{3,2,1,0:T(2,128)S(1)} %get-tuple-element.59), channel_id=1, source_target_pairs={{2,0},{3,1},{6,4},{7,5},{10,8},{11,9},{14,12},{15,13},{18,16},{19,... | collective-permute-start | bytes 294920 | tf_op jit(solution)/shard_map/ppermute | solution.py:24
  28.6 1.9 copy-start.13
  32.2 5.4 %collective-permute-start.4 = (f32[4,12,36,2]{2,0,3,1:T(4,128)S(1)}, f32[4,12,36,2]{2,0,3,1:T(4,128)}, u32[]{:S(2)}, u32[]{:S(2)}) collective-permute-start(f32[4,12,36,2]{2,0,3,1:T(4,128)S(1)} %copy.24), channel_id=1, source_target_pairs={{0,1},{2,3},{4,5},{6,7},{8,9},{10,11},{12,13},{14,15},{16,17},{18,... | collective-permute-start | bytes 41480 | tf_op jit(solution)/shard_map/ppermute | solution.py:21
  36.3 3.5 %collective-permute-start.5 = (f32[4,12,36,2]{2,0,3,1:T(4,128)}, f32[4,12,36,2]{2,0,3,1:T(4,128)}, u32[]{:S(2)}, u32[]{:S(2)}) collective-permute-start(f32[4,12,36,2]{2,0,3,1:T(4,128)} %copy.25), channel_id=1, source_target_pairs={{1,0},{3,2},{5,4},{7,6},{9,8},{11,10},{13,12},{15,14},{17,16},{19,... | collective-permute-start | bytes 41480 | tf_op jit(solution)/shard_map/ppermute | solution.py:24
  48.8 1.3 copy-start.15
  49.9 29.5 %copy-start.6 = (f32[1,8,32,256]{3,2,1,0:T(8,128)}, f32[1,8,32,256]{3,2,1,0:T(8,128)S(1)}, u32[]{:S(2)}) copy-start(f32[1,8,32,256]{3,2,1,0:T(8,128)S(1)} %get-tuple-element.71) | copy-start | bytes 786436
  49.9 29.5 %copy-start.8 = (f32[1,8,32,256]{3,2,1,0:T(8,128)}, f32[1,8,32,256]{3,2,1,0:T(8,128)S(1)}, u32[]{:S(2)}) copy-start(f32[1,8,32,256]{3,2,1,0:T(8,128)S(1)} %get-tuple-element.72) | copy-start | bytes 786436
  50.0 29.5 %copy-start.10 = (f32[1,8,32,256]{3,2,1,0:T(8,128)}, f32[1,8,32,256]{3,2,1,0:T(8,128)S(1)}, u32[]{:S(2)}) copy-start(f32[1,8,32,256]{3,2,1,0:T(8,128)S(1)} %get-tuple-element.73) | copy-start | bytes 786436
  50.1 30.2 %copy-start.2 = (f32[3,8,32,256]{3,2,1,0:T(8,128)}, f32[3,8,32,256]{3,2,1,0:T(8,128)S(1)}, u32[]{:S(2)}) copy-start(f32[3,8,32,256]{3,2,1,0:T(8,128)S(1)} %fusion.4) | copy-start | bytes 2359300
  80.3 9.7 %collective-permute-start.6 = (f32[4,2,32,256]{3,2,1,0:T(8,128)}, f32[4,2,32,256]{3,2,1,0:T(8,128)S(1)}, u32[]{:S(2)}, u32[]{:S(2)}) collective-permute-start(f32[4,2,32,256]{3,2,1,0:T(8,128)} %get-tuple-element.64), channel_id=1, source_target_pairs={{0,4},{4,8},{8,12},{1,5},{5,9},{9,13},{2,6},{6,10},{10,14},{3,7},{... | collective-permute-start | bytes 786440 | tf_op jit(solution)/shard_map/ppermute | solution.py:21
  83.8 10.9 %collective-permute-start.7 = (f32[4,2,32,256]{3,2,1,0:T(8,128)}, f32[4,2,32,256]{3,2,1,0:T(8,128)}, u32[]{:S(2)}, u32[]{:S(2)}) collective-permute-start(f32[4,2,32,256]{3,2,1,0:T(8,128)} %get-tuple-element.65), channel_id=1, source_target_pairs={{4,0},{8,4},{12,8},{5,1},{9,5},{13,9},{6,2},{10,6},{14,10},{7,3},{... | collective-permute-start | bytes 786440 | tf_op jit(solution)/shard_map/ppermute | solution.py:24
  95.9 4.1 %collective-permute-start.8 = (f32[4,12,2,256]{3,2,1,0:T(2,128)S(1)}, f32[4,12,2,256]{3,2,1,0:T(2,128)S(1)}, u32[]{:S(2)}, u32[]{:S(2)}) collective-permute-start(f32[4,12,2,256]{3,2,1,0:T(2,128)S(1)} %get-tuple-element.56), channel_id=1, source_target_pairs={{0,2},{1,3},{4,6},{5,7},{8,10},{9,11},{12,14},{13,15},{16,18},{17,... | collective-permute-start | bytes 294920 | tf_op jit(solution)/shard_map/ppermute | solution.py:21
  97.4 6.7 %collective-permute-start.9 = (f32[4,12,2,256]{3,2,1,0:T(2,128)S(1)}, f32[4,12,2,256]{3,2,1,0:T(2,128)S(1)}, u32[]{:S(2)}, u32[]{:S(2)}) collective-permute-start(f32[4,12,2,256]{3,2,1,0:T(2,128)S(1)} %get-tuple-element.57), channel_id=1, source_target_pairs={{2,0},{3,1},{6,4},{7,5},{10,8},{11,9},{14,12},{15,13},{18,16},{19,... | collective-permute-start | bytes 294920 | tf_op jit(solution)/shard_map/ppermute | solution.py:24
  104.1 3.1 %copy-start.12 = (f32[4,12,2,256]{3,2,1,0:T(2,128)}, f32[4,12,2,256]{3,2,1,0:T(2,128)S(1)}, u32[]{:S(2)}) copy-start(f32[4,12,2,256]{3,2,1,0:T(2,128)S(1)} %collective-permute-done.9) | copy-start | bytes 294916
  108.8 8.1 %collective-permute-start.10 = (f32[4,12,36,2]{2,0,3,1:T(4,128)S(1)}, f32[4,12,36,2]{2,0,3,1:T(4,128)}, u32[]{:S(2)}, u32[]{:S(2)}) collective-permute-start(f32[4,12,36,2]{2,0,3,1:T(4,128)S(1)} %copy.28), channel_id=1, source_target_pairs={{0,1},{2,3},{4,5},{6,7},{8,9},{10,11},{12,13},{14,15},{16,17},{18,... | collective-permute-start | bytes 41480 | tf_op jit(solution)/shard_map/ppermute | solution.py:21
  113.0 6.2 %collective-permute-start.11 = (f32[4,12,36,2]{2,0,3,1:T(4,128)}, f32[4,12,36,2]{2,0,3,1:T(4,128)}, u32[]{:S(2)}, u32[]{:S(2)}) collective-permute-start(f32[4,12,36,2]{2,0,3,1:T(4,128)} %copy.29), channel_id=1, source_target_pairs={{1,0},{3,2},{5,4},{7,6},{9,8},{11,10},{13,12},{15,14},{17,16},{19,... | collective-permute-start | bytes 41480 | tf_op jit(solution)/shard_map/ppermute | solution.py:24
  124.9 3.8 %copy-start.3 = (f32[12,36,260]{2,1,0:T(8,128)}, f32[12,36,260]{2,1,0:T(8,128)S(1)}, u32[]{:S(2)}) copy-start(f32[12,36,260]{2,1,0:T(8,128)S(1)} %get-tuple-element.33) | copy-start | bytes 1347844
  130.8 1.2 copy-start.7
  130.8 1.2 copy-start.9
  130.8 1.2 copy-start.11
  132.0 1.6 copy-start.14
  132.0 1.6 copy-start.16
  133.1 62.5 %copy-start.4 = (f32[12,36,260]{2,1,0:T(8,128)S(1)}, f32[12,36,260]{2,1,0:T(8,128)}, u32[]{:S(2)}) copy-start(f32[12,36,260]{2,1,0:T(8,128)} %copy-done.3) | copy-start | bytes 1347844
where the time goes:
time: 228 us; the launch traced here: 227 us
  other arithmetic  89.2 us (39%)
  blocking collectives  60.5 us (27%)
  waiting for transfers between devices  27.4 us (12%)
  starting transfers between devices  24.9 us (11%)
  local copies, waits for them, and re-layouts  21.7 us (10%)
    psum x1, blocking collectives, local(): readings = lax.psum(partial_sum, ('slab', 'pencil', 'comp'))  60.5 us
    add x1, other arithmetic, advance(): damage_core + TIME_DAMAGE * (2.0 * (1.0 - damage_core) * energy - toughne...  31 us
    broadcast_in_dim x2, other arithmetic, local(): stacked = jnp.concatenate([moved, damage[None]], axis=0)  30.5 us
    ppermute x6, waiting for transfers between devices, with_halo(): lax.ppermute(lax.slice_in_dim(block, 0, width, axis=dim), axis, backward)  17.3 us
    ppermute x6, starting transfers between devices, with_halo(): lax.ppermute(lax.slice_in_dim(block, block.shape[dim] - width, None, axis...  17.2 us
    ppermute x6, waiting for transfers between devices, with_halo(): lax.ppermute(lax.slice_in_dim(block, block.shape[dim] - width, None, axis...  10.2 us
    mul x4, other arithmetic, advance(): total_force = total_force + central(degrade * stress, direction)  9.3 us
    concatenate x4, other arithmetic, with_halo(): block = jnp.concatenate([low, block, high], axis=dim)  8.23 us
  transfers between devices with their start and end apart: 12, of which 8 were waited for; matrix products, arithmetic and copies ran while one was open for 6% of the time, Pallas kernels for 0%

commit v1 on v0

--- a/solution.py
+++ b/solution.py
@@ -141,7 +141,7 @@
     picks = (block_ids[:, None] == sensor_cell[None, :]).astype(jnp.bfloat16)
     point = jnp.dot(pooled, picks, preferred_element_type=jnp.float32)
     partial_sum = dense + POINT_GAIN * point
-    readings = lax.psum(partial_sum, ("slab", "pencil", "comp"))
+    readings = lax.psum(lax.psum(partial_sum, "slab"), ("pencil", "comp"))
     return (moved, damage, readings)
 
 

time: 228 us -> 198 us (0.87)
  blocking collectives: 60.5 us -> 31 us
    psum x1 -> x2, blocking collectives: 60.5 us -> 31 us  [local(): readings = lax.psum(lax.psum(partial_sum, 'slab'), ('pencil', 'comp'))]
where the time goes in v1:
time: 198 us; the launch traced here: 197 us
  other arithmetic  89.2 us (45%)
  blocking collectives  31 us (16%)
  waiting for transfers between devices  27.4 us (14%)
  starting transfers between devices  24.9 us (13%)
  local copies, waits for them, and re-layouts  21.6 us (11%)
    add x1, other arithmetic, advance(): damage_core + TIME_DAMAGE * (2.0 * (1.0 - damage_core) * energy - toughne...  31 us
    psum x2, blocking collectives, local(): readings = lax.psum(lax.psum(partial_sum, 'slab'), ('pencil', 'comp'))  31 us
    broadcast_in_dim x2, other arithmetic, local(): stacked = jnp.concatenate([moved, damage[None]], axis=0)  30.5 us
    ppermute x6, waiting for transfers between devices, with_halo(): lax.ppermute(lax.slice_in_dim(block, 0, width, axis=dim), axis, backward)  17.3 us
    ppermute x6, starting transfers between devices, with_halo(): lax.ppermute(lax.slice_in_dim(block, block.shape[dim] - width, None, axis...  17.2 us
    ppermute x6, waiting for transfers between devices, with_halo(): lax.ppermute(lax.slice_in_dim(block, block.shape[dim] - width, None, axis...  10.2 us
    mul x4, other arithmetic, advance(): total_force = total_force + central(degrade * stress, direction)  9.29 us
    concatenate x4, other arithmetic, with_halo(): block = jnp.concatenate([low, block, high], axis=dim)  8.23 us
  transfers between devices with their start and end apart: 12, of which 8 were waited for; matrix products, arithmetic and copies ran while one was open for 6% of the time, Pallas kernels for 0%

profile of v1, /device:TPU:0, one launch (start us, length us, event | category | flops | bytes accessed | tf_op | source)
XLA Modules:
  0.0 196.9 jit_solution(15091371741418481414)
XLA Ops:
  2.9 5.0 %collective-permute-start = (f32[4,2,32,256]{3,2,1,0:T(8,128)S(1)}, f32[4,2,32,256]{3,2,1,0:T(8,128)S(1)}, u32[]{:S(2)}, u32[]{:S(2)}) collective-permute-start(f32[4,2,32,256]{3,2,1,0:T(8,128)S(1)} %get-tuple-element.66), channel_id=1, source_target_pairs={{0,4},{4,8},{8,12},{1,5},{5,9},{9,13},{2,6},{6,10},{10,14},{3,7},{... | collective-permute-start | bytes 786440 | tf_op jit(solution)/shard_map/ppermute | solution.py:21
  9.1 4.2 %collective-permute-done = f32[4,2,32,256]{3,2,1,0:T(8,128)S(1)} collective-permute-done((f32[4,2,32,256]{3,2,1,0:T(8,128)S(1)}, f32[4,2,32,256]{3,2,1,0:T(8,128)S(1)}, u32[]{:S(2)}, u32[]{:S(2)}) %collective-permute-start) | collective-permute-done | bytes 262176 | tf_op jit(solution)/shard_map/ppermute | solution.py:21
  13.4 4.1 %collective-permute-done.1 = f32[4,2,32,256]{3,2,1,0:T(8,128)S(1)} collective-permute-done((f32[4,2,32,256]{3,2,1,0:T(8,128)S(1)}, f32[4,2,32,256]{3,2,1,0:T(8,128)S(1)}, u32[]{:S(2)}, u32[]{:S(2)}) %collective-permute-start.1) | collective-permute-done | bytes 262176 | tf_op jit(solution)/shard_map/ppermute | solution.py:24
  18.7 3.4 %collective-permute-start.2 = (f32[4,12,2,256]{3,2,1,0:T(2,128)S(1)}, f32[4,12,2,256]{3,2,1,0:T(2,128)S(1)}, u32[]{:S(2)}, u32[]{:S(2)}) collective-permute-start(f32[4,12,2,256]{3,2,1,0:T(2,128)S(1)} %get-tuple-element.58), channel_id=1, source_target_pairs={{0,2},{1,3},{4,6},{5,7},{8,10},{9,11},{12,14},{13,15},{16,18},{17,... | collective-permute-start | bytes 294920 | tf_op jit(solution)/shard_map/ppermute | solution.py:21
  24.3 4.3 %collective-permute-done.3 = f32[4,12,2,256]{3,2,1,0:T(2,128)S(1)} collective-permute-done((f32[4,12,2,256]{3,2,1,0:T(2,128)S(1)}, f32[4,12,2,256]{3,2,1,0:T(2,128)S(1)}, u32[]{:S(2)}, u32[]{:S(2)}) %collective-permute-start.3) | collective-permute-done | bytes 98336 | tf_op jit(solution)/shard_map/ppermute | solution.py:24
  28.9 1.6 fusion.80
  30.5 1.6 copy.24
  32.1 1.9 collective-permute-start.4
  34.0 2.2 %copy.25 = f32[4,12,36,2]{2,0,3,1:T(4,128)} copy(f32[4,12,36,2]{3,2,1,0:T(8,128)} %get-tuple-element.55) | data formatting | bytes 27648 | tf_op jit(solution)/shard_map/slice | solution.py:24
  37.6 2.2 %copy.26 = f32[4,12,36,2]{3,2,1,0:T(8,128)} copy(f32[4,12,36,2]{2,0,3,1:T(4,128)} %collective-permute-done.4) | data formatting | bytes 27648 | tf_op jit(solution)/shard_map/ppermute | solution.py:21
  39.8 2.2 %copy.27 = f32[4,12,36,2]{3,2,1,0:T(8,128)} copy(f32[4,12,36,2]{2,0,3,1:T(4,128)} %collective-permute-done.5) | data formatting | bytes 27648 | tf_op jit(solution)/shard_map/ppermute | solution.py:24
  42.0 3.1 %pad_maximum_fusion = f32[4,12,36,260]{3,2,1,0:T(8,128)S(1)} fusion(f32[4,12,36,2]{3,2,1,0:T(8,128)} %copy.27, f32[4,12,2,256]{3,2,1,0:T(2,128)} %copy-done.13, f32[4,2,32,256]{3,2,1,0:T(8,128)} %copy-done.5, f32[1,8,32,256]{3,2,1,0:T(8,128)S(1)} %multiply_bitcast_fusion, f32[3,8,32,256]{3,2,1,0:T(8,128)S(1)} %copy-done.1, ...), kind=kLoop, calls=%fused_computation.3 | loop fusion | flops 3144960 | bytes 3594240 | tf_op jit(solution)/shard_map/concatenate | solution.py:25
  45.3 2.2 %multiply_multiply_fusion.5 = (f32[10,34,258]{2,1,0:T(8,128)S(1)}, f32[10,34,258]{2,1,0:T(8,128)S(1)}, f32[10,34,258]{2,1,0:T(8,128)S(1)}, f32[10,34,258]{2,1,0:...) fusion(f32[12,36,260]{2,1,0:T(8,128)S(1)} %get-tuple-element.37, ...), kind=kLoop, calls=%fused_computation.68 | loop fusion | flops 2456160 | bytes 8421120 | tf_op jit(solution)/shard_map/mul | solution.py:106
  50.1 29.3 %fusion.51 = f32[1,8,32,256]{3,2,1,0:T(8,128)S(1)} fusion(f32[8,32,256]{2,1,0:T(8,128)S(1)} %copy-done.15, f32[12,36,260]{2,1,0:T(8,128)S(1)} %get-tuple-element.37, f32[10,34,258]{2,1,0:T(8,128)S(1)} %get-tuple-element.46, f32[10,34,258]{2,1,0:T(8,128)S(1)} %get-tuple-element.47, f32[10,34,258]{2,1,0:T(8,128)S(1)} %get-tuple-element.29, ...), kind=kLoop, calls=%fused_computation.127 | loop fusion | flops 23068672 | bytes 4194304 | tf_op jit(solution)/shard_map/broadcast_in_dim | solution.py:128
  80.3 3.5 %collective-permute-start.6 = (f32[4,2,32,256]{3,2,1,0:T(8,128)}, f32[4,2,32,256]{3,2,1,0:T(8,128)S(1)}, u32[]{:S(2)}, u32[]{:S(2)}) collective-permute-start(f32[4,2,32,256]{3,2,1,0:T(8,128)} %get-tuple-element.64), channel_id=1, source_target_pairs={{0,4},{4,8},{8,12},{1,5},{5,9},{9,13},{2,6},{6,10},{10,14},{3,7},{... | collective-permute-start | bytes 786440 | tf_op jit(solution)/shard_map/ppermute | solution.py:21
  85.6 4.4 %collective-permute-done.6 = f32[4,2,32,256]{3,2,1,0:T(8,128)S(1)} collective-permute-done((f32[4,2,32,256]{3,2,1,0:T(8,128)}, f32[4,2,32,256]{3,2,1,0:T(8,128)S(1)}, u32[]{:S(2)}, u32[]{:S(2)}) %collective-permute-start.6) | collective-permute-done | bytes 262176 | tf_op jit(solution)/shard_map/ppermute | solution.py:21
  90.0 4.7 %collective-permute-done.7 = f32[4,2,32,256]{3,2,1,0:T(8,128)} collective-permute-done((f32[4,2,32,256]{3,2,1,0:T(8,128)}, f32[4,2,32,256]{3,2,1,0:T(8,128)}, u32[]{:S(2)}, u32[]{:S(2)}) %collective-permute-start.7) | collective-permute-done | bytes 262176 | tf_op jit(solution)/shard_map/ppermute | solution.py:24
  95.8 1.5 collective-permute-start.8
  99.9 4.1 %collective-permute-done.9 = f32[4,12,2,256]{3,2,1,0:T(2,128)S(1)} collective-permute-done((f32[4,12,2,256]{3,2,1,0:T(2,128)S(1)}, f32[4,12,2,256]{3,2,1,0:T(2,128)S(1)}, u32[]{:S(2)}, u32[]{:S(2)}) %collective-permute-start.9) | collective-permute-done | bytes 98336 | tf_op jit(solution)/shard_map/ppermute | solution.py:24
  104.0 1.5 pad_maximum_fusion.3
  105.6 1.6 fusion.79
  107.2 1.6 copy.28
  108.8 1.9 collective-permute-start.10
  110.7 2.2 %copy.29 = f32[4,12,36,2]{2,0,3,1:T(4,128)} copy(f32[4,12,36,2]{3,2,1,0:T(8,128)} %get-tuple-element.53) | data formatting | bytes 27648 | tf_op jit(solution)/shard_map/slice | solution.py:24
  116.8 2.2 %copy.30 = f32[4,12,36,2]{3,2,1,0:T(8,128)} copy(f32[4,12,36,2]{2,0,3,1:T(4,128)} %collective-permute-done.10) | data formatting | bytes 27648 | tf_op jit(solution)/shard_map/ppermute | solution.py:21
  119.1 2.2 %copy.31 = f32[4,12,36,2]{3,2,1,0:T(8,128)} copy(f32[4,12,36,2]{2,0,3,1:T(4,128)} %collective-permute-done.11) | data formatting | bytes 27648 | tf_op jit(solution)/shard_map/ppermute | solution.py:24
  121.2 3.3 %pad_maximum_fusion.1 = f32[4,12,36,260]{3,2,1,0:T(8,128)S(1)} fusion(f32[4,12,36,2]{3,2,1,0:T(8,128)} %copy.31, f32[4,12,2,256]{3,2,1,0:T(2,128)} %copy-done.12, f32[4,2,32,256]{3,2,1,0:T(8,128)} %collective-permute-done.7, f32[1,8,32,256]{3,2,1,0:T(8,128)S(1)} %fusion.51, f32[3,8,32,256]{3,2,1,0:T(8,128)} %copy-done.2, ...), kind=kLoop, calls=%fused_computation.4 | loop fusion | flops 3144960 | bytes 3594240 | tf_op jit(solution)/shard_map/concatenate | solution.py:25
  124.8 3.8 %multiply_multiply_fusion.2 = (f32[10,34,258]{2,1,0:T(8,128)S(1)}, f32[10,34,258]{2,1,0:T(8,128)}, f32[10,34,258]{2,1,0:T(8,128)S(1)}, f32[10,34,258]{2,1,0:T(8,...) fusion(f32[12,36,260]{2,1,0:T(8,128)S(1)} %get-tuple-element.33, ...), kind=kLoop, calls=%fused_computation.61 | loop fusion | flops 2456160 | bytes 8421120 | tf_op jit(solution)/shard_map/mul | solution.py:106
  128.6 2.1 %multiply_multiply_fusion = (f32[10,34,258]{2,1,0:T(8,128)S(1)}, f32[10,34,258]{2,1,0:T(8,128)}, f32[10,34,258]{2,1,0:T(8,128)S(1)}, f32[10,34,258]{2,1,0:T(8,128)S(1)}) fusion(f32[12,36,260]{2,1,0:T(8,128)S(1)} %get-tuple-element.33, f32[12,36,260]{2,1,0:T(8,128)S(1)} %get-tuple-element.30, f32[12,36,260]{2,1,0:T(8,128)S(1)} %get-tuple-element.31, ...), kind=kLoop, calls=%fused_computation.58 | loop fusion | flops 1666680 | bytes 4912320 | tf_op jit(solution)/shard_map/mul | solution.py:106
  134.8 19.0 %psum.14 = f32[3,4096]{1,0:T(4,128)} all-reduce(f32[3,4096]{1,0:T(4,128)} %fusion), channel_id=1, replica_groups=mesh['groups'=2,'slab'=4,'pencil'=2,'comp'=2] {'slab'}, use_global_device_ids=true, to_apply=%region_1.0 | all-reduce | flops 12288 | bytes 98304 | tf_op jit(solution)/shard_map/psum | solution.py:144
  153.9 12.0 %psum.15 = f32[3,4096]{1,0:T(4,128)} all-reduce(f32[3,4096]{1,0:T(4,128)} %psum.14), channel_id=1, replica_groups=mesh['groups'=2,'slab'=4,'pencil'=2,'comp'=2] {'pencil','comp'}, use_global_device_ids=true, to_apply=%region_2.0 | all-reduce | flops 12288 | bytes 98304 | tf_op jit(solution)/shard_map/psum | solution.py:144
  165.8 31.0 %fusion.26 = f32[8,32,256]{2,1,0:T(8,128)} fusion(f32[8,32,256]{2,1,0:T(8,128)} %param.6, f32[12,36,260]{2,1,0:T(8,128)S(1)} %copy-done.4, f32[10,34,258]{2,1,0:T(8,128)S(1)} %get-tuple-element.39, f32[10,34,258]{2,1,0:T(8,128)} %get-tuple-element.40, f32[10,34,258]{2,1,0:T(8,128)} %get-tuple-element.18, f32[10,34,258]{2,1,0:T(8,128)} %get-tuple-element.44, ...), kind=kLoop, calls=%fused_computation.82 | loop fusion | flops 23068672 | bytes 4194304 | tf_op jit(solution)/shard_map/add | solution.py:115
  (67 shorter events, 25.7 us)
Async XLA Ops:
  0.6 132.4 %copy-start = (bf16[8,32,1,4096]{3,1,2,0:T(8,128)(2,1)S(1)}, bf16[8,32,1,4096]{3,1,2,0:T(8,128)(2,1)}, u32[]{:S(2)}) copy-start(bf16[8,32,1,4096]{3,1,2,0:T(8,128)(2,1)} %param.8) | copy-start | bytes 6291460
  0.6 28.0 %copy-start.1 = (f32[3,8,32,256]{3,2,1,0:T(8,128)S(1)}, f32[3,8,32,256]{3,2,1,0:T(8,128)}, u32[]{:S(2)}) copy-start(f32[3,8,32,256]{3,2,1,0:T(8,128)} %param.5) | copy-start | bytes 2359300
  2.9 10.5 %collective-permute-start = (f32[4,2,32,256]{3,2,1,0:T(8,128)S(1)}, f32[4,2,32,256]{3,2,1,0:T(8,128)S(1)}, u32[]{:S(2)}, u32[]{:S(2)}) collective-permute-start(f32[4,2,32,256]{3,2,1,0:T(8,128)S(1)} %get-tuple-element.66), channel_id=1, source_target_pairs={{0,4},{4,8},{8,12},{1,5},{5,9},{9,13},{2,6},{6,10},{10,14},{3,7},{... | collective-permute-start | bytes 786440 | tf_op jit(solution)/shard_map/ppermute | solution.py:21
  7.8 9.7 %collective-permute-start.1 = (f32[4,2,32,256]{3,2,1,0:T(8,128)S(1)}, f32[4,2,32,256]{3,2,1,0:T(8,128)S(1)}, u32[]{:S(2)}, u32[]{:S(2)}) collective-permute-start(f32[4,2,32,256]{3,2,1,0:T(8,128)S(1)} %get-tuple-element.67), channel_id=1, source_target_pairs={{4,0},{8,4},{12,8},{5,1},{9,5},{13,9},{6,2},{10,6},{14,10},{7,3},{... | collective-permute-start | bytes 786440 | tf_op jit(solution)/shard_map/ppermute | solution.py:24
  17.5 13.0 %copy-start.5 = (f32[4,2,32,256]{3,2,1,0:T(8,128)}, f32[4,2,32,256]{3,2,1,0:T(8,128)S(1)}, u32[]{:S(2)}) copy-start(f32[4,2,32,256]{3,2,1,0:T(8,128)S(1)} %collective-permute-done.1) | copy-start | bytes 786436
  18.7 5.6 %collective-permute-start.2 = (f32[4,12,2,256]{3,2,1,0:T(2,128)S(1)}, f32[4,12,2,256]{3,2,1,0:T(2,128)S(1)}, u32[]{:S(2)}, u32[]{:S(2)}) collective-permute-start(f32[4,12,2,256]{3,2,1,0:T(2,128)S(1)} %get-tuple-element.58), channel_id=1, source_target_pairs={{0,2},{1,3},{4,6},{5,7},{8,10},{9,11},{12,14},{13,15},{16,18},{17,... | collective-permute-start | bytes 294920 | tf_op jit(solution)/shard_map/ppermute | solution.py:21
  22.1 6.5 %collective-permute-start.3 = (f32[4,12,2,256]{3,2,1,0:T(2,128)S(1)}, f32[4,12,2,256]{3,2,1,0:T(2,128)S(1)}, u32[]{:S(2)}, u32[]{:S(2)}) collective-permute-start(f32[4,12,2,256]{3,2,1,0:T(2,128)S(1)} %get-tuple-element.59), channel_id=1, source_target_pairs={{2,0},{3,1},{6,4},{7,5},{10,8},{11,9},{14,12},{15,13},{18,16},{19,... | collective-permute-start | bytes 294920 | tf_op jit(solution)/shard_map/ppermute | solution.py:24
  28.6 1.9 copy-start.13
  32.1 5.4 %collective-permute-start.4 = (f32[4,12,36,2]{2,0,3,1:T(4,128)S(1)}, f32[4,12,36,2]{2,0,3,1:T(4,128)}, u32[]{:S(2)}, u32[]{:S(2)}) collective-permute-start(f32[4,12,36,2]{2,0,3,1:T(4,128)S(1)} %copy.24), channel_id=1, source_target_pairs={{0,1},{2,3},{4,5},{6,7},{8,9},{10,11},{12,13},{14,15},{16,17},{18,... | collective-permute-start | bytes 41480 | tf_op jit(solution)/shard_map/ppermute | solution.py:21
  36.3 3.5 %collective-permute-start.5 = (f32[4,12,36,2]{2,0,3,1:T(4,128)}, f32[4,12,36,2]{2,0,3,1:T(4,128)}, u32[]{:S(2)}, u32[]{:S(2)}) collective-permute-start(f32[4,12,36,2]{2,0,3,1:T(4,128)} %copy.25), channel_id=1, source_target_pairs={{1,0},{3,2},{5,4},{7,6},{9,8},{11,10},{13,12},{15,14},{17,16},{19,... | collective-permute-start | bytes 41480 | tf_op jit(solution)/shard_map/ppermute | solution.py:24
  48.7 1.3 copy-start.15
  49.9 29.5 %copy-start.6 = (f32[1,8,32,256]{3,2,1,0:T(8,128)}, f32[1,8,32,256]{3,2,1,0:T(8,128)S(1)}, u32[]{:S(2)}) copy-start(f32[1,8,32,256]{3,2,1,0:T(8,128)S(1)} %get-tuple-element.71) | copy-start | bytes 786436
  49.9 29.5 %copy-start.8 = (f32[1,8,32,256]{3,2,1,0:T(8,128)}, f32[1,8,32,256]{3,2,1,0:T(8,128)S(1)}, u32[]{:S(2)}) copy-start(f32[1,8,32,256]{3,2,1,0:T(8,128)S(1)} %get-tuple-element.72) | copy-start | bytes 786436
  49.9 29.5 %copy-start.10 = (f32[1,8,32,256]{3,2,1,0:T(8,128)}, f32[1,8,32,256]{3,2,1,0:T(8,128)S(1)}, u32[]{:S(2)}) copy-start(f32[1,8,32,256]{3,2,1,0:T(8,128)S(1)} %get-tuple-element.73) | copy-start | bytes 786436
  50.1 30.2 %copy-start.2 = (f32[3,8,32,256]{3,2,1,0:T(8,128)}, f32[3,8,32,256]{3,2,1,0:T(8,128)S(1)}, u32[]{:S(2)}) copy-start(f32[3,8,32,256]{3,2,1,0:T(8,128)S(1)} %fusion.4) | copy-start | bytes 2359300
  80.3 9.7 %collective-permute-start.6 = (f32[4,2,32,256]{3,2,1,0:T(8,128)}, f32[4,2,32,256]{3,2,1,0:T(8,128)S(1)}, u32[]{:S(2)}, u32[]{:S(2)}) collective-permute-start(f32[4,2,32,256]{3,2,1,0:T(8,128)} %get-tuple-element.64), channel_id=1, source_target_pairs={{0,4},{4,8},{8,12},{1,5},{5,9},{9,13},{2,6},{6,10},{10,14},{3,7},{... | collective-permute-start | bytes 786440 | tf_op jit(solution)/shard_map/ppermute | solution.py:21
  83.8 10.9 %collective-permute-start.7 = (f32[4,2,32,256]{3,2,1,0:T(8,128)}, f32[4,2,32,256]{3,2,1,0:T(8,128)}, u32[]{:S(2)}, u32[]{:S(2)}) collective-permute-start(f32[4,2,32,256]{3,2,1,0:T(8,128)} %get-tuple-element.65), channel_id=1, source_target_pairs={{4,0},{8,4},{12,8},{5,1},{9,5},{13,9},{6,2},{10,6},{14,10},{7,3},{... | collective-permute-start | bytes 786440 | tf_op jit(solution)/shard_map/ppermute | solution.py:24
  95.8 4.1 %collective-permute-start.8 = (f32[4,12,2,256]{3,2,1,0:T(2,128)S(1)}, f32[4,12,2,256]{3,2,1,0:T(2,128)S(1)}, u32[]{:S(2)}, u32[]{:S(2)}) collective-permute-start(f32[4,12,2,256]{3,2,1,0:T(2,128)S(1)} %get-tuple-element.56), channel_id=1, source_target_pairs={{0,2},{1,3},{4,6},{5,7},{8,10},{9,11},{12,14},{13,15},{16,18},{17,... | collective-permute-start | bytes 294920 | tf_op jit(solution)/shard_map/ppermute | solution.py:21
  97.4 6.7 %collective-permute-start.9 = (f32[4,12,2,256]{3,2,1,0:T(2,128)S(1)}, f32[4,12,2,256]{3,2,1,0:T(2,128)S(1)}, u32[]{:S(2)}, u32[]{:S(2)}) collective-permute-start(f32[4,12,2,256]{3,2,1,0:T(2,128)S(1)} %get-tuple-element.57), channel_id=1, source_target_pairs={{2,0},{3,1},{6,4},{7,5},{10,8},{11,9},{14,12},{15,13},{18,16},{19,... | collective-permute-start | bytes 294920 | tf_op jit(solution)/shard_map/ppermute | solution.py:24
  104.0 3.1 %copy-start.12 = (f32[4,12,2,256]{3,2,1,0:T(2,128)}, f32[4,12,2,256]{3,2,1,0:T(2,128)S(1)}, u32[]{:S(2)}) copy-start(f32[4,12,2,256]{3,2,1,0:T(2,128)S(1)} %collective-permute-done.9) | copy-start | bytes 294916
  108.8 8.1 %collective-permute-start.10 = (f32[4,12,36,2]{2,0,3,1:T(4,128)S(1)}, f32[4,12,36,2]{2,0,3,1:T(4,128)}, u32[]{:S(2)}, u32[]{:S(2)}) collective-permute-start(f32[4,12,36,2]{2,0,3,1:T(4,128)S(1)} %copy.28), channel_id=1, source_target_pairs={{0,1},{2,3},{4,5},{6,7},{8,9},{10,11},{12,13},{14,15},{16,17},{18,... | collective-permute-start | bytes 41480 | tf_op jit(solution)/shard_map/ppermute | solution.py:21
  112.9 6.1 %collective-permute-start.11 = (f32[4,12,36,2]{2,0,3,1:T(4,128)}, f32[4,12,36,2]{2,0,3,1:T(4,128)}, u32[]{:S(2)}, u32[]{:S(2)}) collective-permute-start(f32[4,12,36,2]{2,0,3,1:T(4,128)} %copy.29), channel_id=1, source_target_pairs={{1,0},{3,2},{5,4},{7,6},{9,8},{11,10},{13,12},{15,14},{17,16},{19,... | collective-permute-start | bytes 41480 | tf_op jit(solution)/shard_map/ppermute | solution.py:24
  124.8 3.8 %copy-start.3 = (f32[12,36,260]{2,1,0:T(8,128)}, f32[12,36,260]{2,1,0:T(8,128)S(1)}, u32[]{:S(2)}) copy-start(f32[12,36,260]{2,1,0:T(8,128)S(1)} %get-tuple-element.33) | copy-start | bytes 1347844
  130.7 1.2 copy-start.7
  130.7 1.2 copy-start.9
  130.7 1.2 copy-start.11
  131.8 1.6 copy-start.14
  131.8 1.6 copy-start.16
  132.9 32.9 %copy-start.4 = (f32[12,36,260]{2,1,0:T(8,128)S(1)}, f32[12,36,260]{2,1,0:T(8,128)}, u32[]{:S(2)}) copy-start(f32[12,36,260]{2,1,0:T(8,128)} %copy-done.3) | copy-start | bytes 1347844
